TPU v7x, 32 devices: a whole 2x2x4 slice. The times are simulated.
32 devices in a mesh: row: 4 (over y, x), col: 8 (over z, core).
Axes of the slice: x: 2, y: 2, z: 4, core: 2. Of those that a mesh axis runs over, the one named last changes fastest.
Arguments:
- gate_weight: bfloat16 [4608, 36864], P('row', 'col'), may hold values from -8.838835 to 8.838835
- up_weight: bfloat16 [4608, 36864], P('row', 'col'), may hold values from -8.838835 to 8.838835
- routes: int32 [2, 4], replicated, may hold values from 0 to 3, each once within a row
Outputs:
- gate_serving: bfloat16 [4608, 36864], P('col', 'row')
- up_serving: bfloat16 [4608, 36864], P('col', 'row')
- scales: float32 [2, 36864], P(None, 'row')
Inputs may be any that keep to these rules, and one draw needn't show every extreme that they name: Each row of routes names every serving rank's piece once.
All inputs are finite; a program needn't handle non-finite values. Where the computation divides by a largest or mean magnitude, that divisor is 1e-20 or more.
Results may differ from a plain program's by a relative error of at most 0.001.
Values may be sent and summed in bfloat16 or wider, within the bound.
A program may use at most 128 MiB of HBM per device.

v0:
```python
import functools

import jax
import jax.numpy as jnp
from jax import lax
from jax.experimental import pallas as pl
from jax.experimental.pallas import tpu as pltpu
from jax.sharding import PartitionSpec as P

EPSILON = 1e-06
LIMIT = 4.0
MESH = pl.DeviceIdType.MESH
VMEM_BYTES = 60 * 1024 * 1024
CHUNKS = 4
AHEAD = 2


def column_peaks(weight):
    return jnp.max(jnp.abs(weight), axis=0).astype(jnp.float32)


def quantize(weight, peaks):
    factor = LIMIT / (peaks + EPSILON)
    return (weight.astype(jnp.float32) * factor[None, :]).astype(jnp.bfloat16)


def order_pieces(weight, order, pieces):
    height, width = weight.shape
    shaped = weight.reshape(height, pieces, width // pieces)
    return jnp.take(shaped, order, axis=1).reshape(height, width)


def own_piece(peaks, pick, pieces):
    shaped = ((peaks + EPSILON) / LIMIT).reshape(pieces, -1)
    return lax.dynamic_index_in_dim(shaped, pick, 0, keepdims=False)


def exchange(sent):
    sent = lax.all_to_all(sent, "row", split_axis=1, concat_axis=0, tiled=True)
    return lax.all_to_all(sent, "col", split_axis=0, concat_axis=1, tiled=True)


def plain_shards(gate_weight, up_weight, routes):
    pieces = lax.axis_size("row")
    row_index = lax.axis_index("row")
    gate_peaks, up_peaks = lax.pmax((column_peaks(gate_weight), column_peaks(up_weight)), "row")
    gate_serving = exchange(order_pieces(quantize(gate_weight, gate_peaks), routes[0], pieces))
    up_serving = exchange(order_pieces(quantize(up_weight, up_peaks), routes[1], pieces))
    chosen = jnp.take(routes, row_index, axis=1)
    local_scales = jnp.stack(
        [own_piece(gate_peaks, chosen[0], pieces), own_piece(up_peaks, chosen[1], pieces)]
    )
    scales = lax.all_gather(local_scales, "col", axis=1, tiled=True)
    return (gate_serving, up_serving, scales)


def move_kernel(
    n_row, n_col, depth, parts,
    routes_ref, gate_ref, up_ref, got_ref, peaks_ref,
    rows, sent_ref, mid, tops, peak_ref, peak_mid, peak_own,
    load, send1, recv1, send2, recv2, psend1, precv1, psend2, precv2,
):
    row, col = lax.axis_index("row"), lax.axis_index("col")
    ratio = n_col // n_row
    size = depth // parts
    total = 2 * ratio * parts
    piece = gate_ref.shape[1] // n_row

    barrier = pltpu.get_barrier_semaphore()
    for s in range(1, n_row):
        pl.semaphore_signal(
            barrier, inc=1, device_id=(lax.rem(row + s, n_row), col), device_id_type=MESH
        )
    for s in range(1, n_col):
        pl.semaphore_signal(
            barrier, inc=1, device_id=(row, lax.rem(col + s, n_col)), device_id_type=MESH
        )
    pl.semaphore_wait(barrier, n_row + n_col - 2)

    def place(k):
        p, rest = k // (ratio * parts), k % (ratio * parts)
        q, h = rest // ratio, rest % ratio
        src = pl.ds(pl.multiple_of((p * ratio + h) * depth + q * size, 16), size)
        dst = pl.ds(pl.multiple_of(p * depth + q * size, 16), size)
        return h, p * parts + q, src, dst

    def first(k, s):
        _, _, src, _ = place(k)
        to = lax.rem(row + s, n_row)
        return pltpu.make_async_remote_copy(
            src_ref=sent_ref.at[to, src],
            dst_ref=mid.at[n_row - 1 - s, src],
            send_sem=send1.at[k, s - 1],
            recv_sem=recv1.at[k, s - 1],
            device_id=(to, col),
            device_id_type=MESH,
        )

    def second(k, s):
        h, slot, src, dst = place(k)
        source = lax.rem(row + n_row - s, n_row)
        to = source * ratio + h
        block = sent_ref.at[row, src] if s == 0 else mid.at[n_row - 1 - s, src]
        remote = pltpu.make_async_remote_copy(
            src_ref=block,
            dst_ref=got_ref.at[col, dst],
            send_sem=send2.at[k, s],
            recv_sem=recv2.at[slot, col],
            device_id=(row, to),
            device_id_type=MESH,
        )
        local = pltpu.make_async_copy(block, got_ref.at[col, dst], recv2.at[slot, col])
        return to, remote, local

    def start_second(k, s):
        to, remote, local = second(k, s)

        @pl.when(to != col)
        def _():
            remote.start()

        @pl.when(to == col)
        def _():
            local.start()

    def peak_first(s):
        to = lax.rem(row + s, n_row)
        return pltpu.make_async_remote_copy(
            src_ref=peak_ref.at[to],
            dst_ref=peak_mid.at[s - 1],
            send_sem=psend1.at[s - 1],
            recv_sem=precv1.at[s - 1],
            device_id=(to, col),
            device_id_type=MESH,
        )

    def peak_second(s):
        return pltpu.make_async_remote_copy(
            src_ref=peak_own,
            dst_ref=peaks_ref.at[col],
            send_sem=psend2.at[s - 1],
            recv_sem=precv2.at[s - 1],
            device_id=(row, lax.rem(col + s, n_col)),
            device_id_type=MESH,
        )

    def fetch(k, ref):
        _, _, src, _ = place(k)
        height = ratio * depth
        start = pl.multiple_of(lax.rem(src.start, height), 16)
        slot = lax.rem(k, 2)
        return pltpu.make_async_copy(ref.at[pl.ds(start, size)], rows.at[slot], load.at[slot])

    def start_fetch(k):
        @pl.when(k < total // 2)
        def _():
            fetch(k, gate_ref).start()

        @pl.when(k >= total // 2)
        def _():
            fetch(k, up_ref).start()

    def pick(p, i, pieces):
        chosen = pieces[0]
        for j in range(1, n_row):
            chosen = jnp.where(routes_ref[p, i] == j, pieces[j], chosen)
        return chosen

    def prepare(k):
        fetch(k, gate_ref).wait()
        p, slot = k // (ratio * parts), lax.rem(k, 2)
        _, _, src, _ = place(k)

        @pl.loop(0, size // 16)
        def _(g):
            here = pl.ds(pl.multiple_of(g * 16, 16), 16)
            there = pl.ds(pl.multiple_of(src.start + g * 16, 16), 16)
            pieces = [rows[slot, here, pl.ds(j * piece, piece)] for j in range(n_row)]
            for j in range(n_row):
                cols = pl.ds(j * piece, piece)
                tops[p, :, cols] = jnp.maximum(tops[p, :, cols], jnp.abs(pieces[j]))
            for i in range(n_row):
                sent_ref[i, there, :] = pick(p, i, pieces)

        @pl.when(k + 2 < total)
        def _():
            start_fetch(k + 2)

    def begin(k):
        for s in range(1, n_row):
            first(k, s).start()
        start_second(k, 0)

    tops[...] = jnp.zeros_like(tops)
    start_fetch(0)
    start_fetch(1)
    prepare(0)
    for k in range(AHEAD):
        prepare(k + 1)
        begin(k)

    @pl.loop(0, total)
    def _(k):
        @pl.when(k + AHEAD + 1 < total)
        def _():
            prepare(k + AHEAD + 1)

        @pl.when(k + AHEAD < total)
        def _():
            begin(k + AHEAD)

        @pl.when(k == total - AHEAD - 1)
        def _():
            for p in range(2):
                pieces = [
                    jnp.max(tops[p, :, pl.ds(j * piece, piece)].astype(jnp.float32), axis=0, keepdims=True)
                    for j in range(n_row)
                ]
                for i in range(n_row):
                    peak_ref[i, pl.ds(p, 1), :] = pick(p, i, pieces)

        for s in range(1, n_row):
            first(k, s).wait_recv()
            start_second(k, s)

    def drain(k):
        for s in range(n_row):
            to, remote, _ = second(k, s)

            @pl.when(to != col)
            def _():
                remote.wait_send()

    for s in range(1, n_row):
        peak_first(s).start()

    @pl.loop(0, total)
    def _(k):
        for s in range(1, n_row):
            first(k, s).wait_send()

    top = peak_ref[row]
    for s in range(1, n_row):
        peak_first(s).wait()
        top = jnp.maximum(top, peak_mid[s - 1])
    peak_own[...] = top
    peaks_ref[col] = top

    @pl.loop(0, total * 3 // 4)
    def _(k):
        drain(k)

    for s in range(1, n_col):
        peak_second(s).start()

    @pl.loop(total * 3 // 4, total)
    def _(k):
        drain(k)

    for s in range(1, n_col):
        peak_second(s).wait()

    @pl.loop(0, 2 * parts)
    def _(slot):
        for c in range(n_col):
            block = got_ref.at[c, pl.ds(pl.multiple_of(slot * size, 16), size)]
            pltpu.make_async_copy(block, block, recv2.at[slot, c]).wait()


def move_call(gate_weight, up_weight, routes, n_row, n_col, parts):
    height, width = gate_weight.shape
    kind = gate_weight.dtype
    piece = width // n_row
    ratio = n_col // n_row
    depth = height // ratio
    total = 2 * ratio * parts
    dma = pltpu.SemaphoreType.DMA
    return pl.pallas_call(
        functools.partial(move_kernel, n_row, n_col, depth, parts),
        out_shape=[
            jax.ShapeDtypeStruct((n_col, 2 * depth, piece), kind),
            jax.ShapeDtypeStruct((n_col, 2, piece), jnp.float32),
        ],
        in_specs=[
            pl.BlockSpec(memory_space=pltpu.SMEM),
            pl.BlockSpec(memory_space=pl.ANY),
            pl.BlockSpec(memory_space=pl.ANY),
        ],
        out_specs=[
            pl.BlockSpec(memory_space=pl.ANY),
            pl.BlockSpec(memory_space=pltpu.VMEM),
        ],
        scratch_shapes=[
            pltpu.VMEM((2, depth // parts, width), kind),
            pltpu.VMEM((n_row, 2 * height, piece), kind),
            pltpu.VMEM((n_row - 1, 2 * height, piece), kind),
            pltpu.VMEM((2, 16, width), kind),
            pltpu.VMEM((n_row, 2, piece), jnp.float32),
            pltpu.VMEM((n_row - 1, 2, piece), jnp.float32),
            pltpu.VMEM((2, piece), jnp.float32),
            dma((2,)),
            dma((total, n_row - 1)),
            dma((total, n_row - 1)),
            dma((total, n_row)),
            dma((2 * parts, n_col)),
            dma((n_row - 1,)),
            dma((n_row - 1,)),
            dma((n_col - 1,)),
            dma((n_col - 1,)),
        ],
        compiler_params=pltpu.CompilerParams(
            collective_id=0, has_side_effects=True, vmem_limit_bytes=VMEM_BYTES
        ),
    )(routes, gate_weight, up_weight)


def finish_kernel(got_ref, peaks_ref, gate_ref, up_ref, scales_ref):
    base = peaks_ref[0] + EPSILON
    scales_ref[...] = base / LIMIT
    factor = LIMIT / base
    for p, ref in enumerate((gate_ref, up_ref)):
        block = got_ref[0, p].astype(jnp.float32)
        ref[...] = (block * factor[p][None, :]).astype(ref.dtype)


def finish_call(got, peaks, steps):
    n_col, _, depth, piece = got.shape
    tile = depth // steps
    return pl.pallas_call(
        finish_kernel,
        grid=(n_col, steps),
        in_specs=[
            pl.BlockSpec((1, 2, tile, piece), lambda c, j: (c, 0, j, 0)),
            pl.BlockSpec((1, 2, piece), lambda c, j: (c, 0, 0)),
        ],
        out_specs=[
            pl.BlockSpec((tile, piece), lambda c, j: (j, c)),
            pl.BlockSpec((tile, piece), lambda c, j: (j, c)),
            pl.BlockSpec((2, piece), lambda c, j: (0, c)),
        ],
        out_shape=[
            jax.ShapeDtypeStruct((depth, n_col * piece), got.dtype),
            jax.ShapeDtypeStruct((depth, n_col * piece), got.dtype),
            jax.ShapeDtypeStruct((2, n_col * piece), jnp.float32),
        ],
    )(got, peaks)


def kernel_shards(n_row, n_col, gate_weight, up_weight, routes):
    height = gate_weight.shape[0]
    got, tops = move_call(gate_weight, up_weight, routes, n_row, n_col, CHUNKS)
    piece = got.shape[-1]
    got = got.reshape(n_col, 2, height * n_row // n_col, piece)
    return tuple(finish_call(got, tops, 1))


def fits(n_row, n_col, height, width):
    if n_col % n_row or width % n_row or (width // n_row) % 128:
        return False
    ratio = n_col // n_row
    held_bytes = (2 * n_row - 1) * 2 * height * (width // n_row) * 2
    return height % (ratio * CHUNKS * 16) == 0 and held_bytes < 48 * 1024 * 1024


def solution(mesh):
    n_row, n_col = mesh.shape["row"], mesh.shape["col"]

    def shards(gate_weight, up_weight, routes):
        if fits(n_row, n_col, *gate_weight.shape):
            return kernel_shards(n_row, n_col, gate_weight, up_weight, routes)
        return plain_shards(gate_weight, up_weight, routes)

    return jax.shard_map(
        shards,
        mesh=mesh,
        in_specs=(P("row", "col"), P("row", "col"), P()),
        out_specs=(P("col", "row"), P("col", "row"), P(None, "row")),
        check_vma=False,
    )
```

profile of v0, /device:TPU:5, one launch (start us, length us, event | category | flops | bytes accessed | tf_op | source)
XLA Modules:
  0.0 494.1 jit_solution(8729396680844833015)
XLA Ops:
  0.6 477.1 %shard_map.58 = (bf16[8,1152,1152]{2,1,0:T(8,128)(2,1)}, f32[8,2,1152]{2,1,0:T(2,128)}) custom-call(s32[2,4]{1,0:T(2,128)} %routes_ref.1, bf16[1152,4608]{1,0:T(8,128)(2,1)} %gate_ref.1, bf16[1152,4608]{1,0:T(8,128)(2,1)} %up_ref.1), custom_call_target="tpu_custom_call" | custom-call | tf_op jit(solution)/shard_map/pallas_call | solution.py:278
  477.7 16.3 %shard_map.59 = (bf16[576,9216]{1,0:T(8,128)(2,1)}, bf16[576,9216]{1,0:T(8,128)(2,1)}, f32[2,9216]{1,0:T(2,128)}) custom-call(bf16[8,2,576,1152]{3,2,1,0:T(8,128)(2,1)} %bitcast.1, f32[8,2,1152]{2,1,0:T(2,128)} %get-tuple-element.6.peaks_ref), custom_call_target="tpu_custom_call" | custom-call | tf_op jit(solution)/shard_map/pallas_call | solution.py:329
where the time goes:
time: 497 us; the launch traced here: 494 us
  Pallas kernels  493 us (99%)
    pallas_call x1, Pallas kernels, move_call(): pl.pallas_call(functools.partial(move_kernel, n_row, n_col, depth, parts)...  477 us
    pallas_call x1, Pallas kernels, finish_call(): pl.pallas_call(finish_kernel, grid=(n_col, steps), in_specs=[pl.BlockSpec...  16.3 us

commit v1 on v0

v1 whole, which is shorter than its diff:
```python
import functools

import jax
import jax.numpy as jnp
from jax import lax
from jax.experimental import pallas as pl
from jax.experimental.pallas import tpu as pltpu
from jax.sharding import PartitionSpec as P

EPSILON = 1e-06
LIMIT = 4.0
MESH = pl.DeviceIdType.MESH
MOVE_BYTES = 40 * 1024 * 1024
STORE_BYTES = 1024 * 1024
PARTS = 9
LAG = 2


def column_peaks(weight):
    return jnp.max(jnp.abs(weight), axis=0).astype(jnp.float32)


def quantize(weight, peaks):
    factor = LIMIT / (peaks + EPSILON)
    return (weight.astype(jnp.float32) * factor[None, :]).astype(jnp.bfloat16)


def order_pieces(weight, order, pieces):
    height, width = weight.shape
    shaped = weight.reshape(height, pieces, width // pieces)
    return jnp.take(shaped, order, axis=1).reshape(height, width)


def own_piece(peaks, pick, pieces):
    shaped = ((peaks + EPSILON) / LIMIT).reshape(pieces, -1)
    return lax.dynamic_index_in_dim(shaped, pick, 0, keepdims=False)


def exchange(sent):
    sent = lax.all_to_all(sent, "row", split_axis=1, concat_axis=0, tiled=True)
    return lax.all_to_all(sent, "col", split_axis=0, concat_axis=1, tiled=True)


def plain_shards(gate_weight, up_weight, routes):
    pieces = lax.axis_size("row")
    row_index = lax.axis_index("row")
    gate_peaks, up_peaks = lax.pmax((column_peaks(gate_weight), column_peaks(up_weight)), "row")
    gate_serving = exchange(order_pieces(quantize(gate_weight, gate_peaks), routes[0], pieces))
    up_serving = exchange(order_pieces(quantize(up_weight, up_peaks), routes[1], pieces))
    chosen = jnp.take(routes, row_index, axis=1)
    local_scales = jnp.stack(
        [own_piece(gate_peaks, chosen[0], pieces), own_piece(up_peaks, chosen[1], pieces)]
    )
    scales = lax.all_gather(local_scales, "col", axis=1, tiled=True)
    return (gate_serving, up_serving, scales)


def move_kernel(
    n_row, n_col, depth, size, head,
    routes_ref, gate_ref, up_ref, got_ref, scales_ref,
    sent, mid, tops, peak, peak_mid, total, factor, peak_all,
    load, send1, recv1, send2, recv2, psend1, precv1, psend2, precv2,
):
    row, col = lax.axis_index("row"), lax.axis_index("col")
    ratio = n_col // n_row
    height = ratio * depth
    piece = sent.shape[2]
    slots = depth // size
    heads = [(h, q, n) for q, n in head for h in range(ratio)]
    steps = (2 * slots - 1) * ratio
    mine = row * ratio

    def peer_row(s):
        return lax.rem(row + s, n_row)

    def peer_col(s):
        return lax.rem(col + s, n_col)

    def local(ref, target, sem):
        return pltpu.make_async_copy(ref, target, sem)

    def remote(ref, target, send, recv, to_row, to_col):
        return pltpu.make_async_remote_copy(
            src_ref=ref, dst_ref=target, send_sem=send, recv_sem=recv,
            device_id=(to_row, to_col), device_id_type=MESH,
        )

    def fetch(p, h, start, n, index):
        ref = (gate_ref, up_ref)[p]
        for j in range(n_row):
            local(
                ref.at[pl.ds(h * depth + start, n), pl.ds(j * piece, piece)],
                sent.at[j, pl.ds(p * height + h * depth + start, n)],
                load.at[index],
            ).start()

    def fetched(p, h, start, n, index):
        block = sent.at[:, pl.ds(p * height + h * depth + start, n)]
        local(block, block, load.at[index]).wait()

    def rows_of(h, p, start, n):
        src = pl.ds(pl.multiple_of((p * ratio + h) * depth + start, 16), n)
        dst = pl.ds(pl.multiple_of(p * depth + start, 16), n)
        return src, dst

    def start_first(index, h, p, start, n):
        src, dst = rows_of(h, p, start, n)
        for s in range(1, n_row):
            to = peer_row(s)

            @pl.when(mine + h != col)
            def _():
                remote(
                    sent.at[to, src], mid.at[n_row - 1 - s, src],
                    send1.at[s - 1], recv1.at[index, s - 1], to, col,
                ).start()

            @pl.when(mine + h == col)
            def _():
                remote(
                    sent.at[to, src], got_ref.at[col, dst],
                    send1.at[s - 1], recv1.at[index, s - 1], to, col,
                ).start()

    def start_second(s, h, p, start, n, kind):
        src, dst = rows_of(h, p, start, n)
        to = peer_row(n_row - s) * ratio + h
        block = sent.at[row, src] if s == 0 else mid.at[n_row - 1 - s, src]

        @pl.when(to != col)
        def _():
            remote(block, got_ref.at[col, dst], send2.at[s], recv2.at[kind, col], row, to).start()

        if s == 0:
            @pl.when(to == col)
            def _():
                @pl.loop(0, n // 16)
                def _(g):
                    here = pl.ds(pl.multiple_of(src.start + g * 16, 16), 16)
                    there = pl.ds(pl.multiple_of(dst.start + g * 16, 16), 16)
                    got_ref[col, there, :] = sent[row, here, :]

    def forward(index, h, p, start, n, kind):
        src, _ = rows_of(h, p, start, n)
        for s in range(1, n_row):
            block = mid.at[n_row - 1 - s, src]
            local(block, block, recv1.at[index, s - 1]).wait()
            start_second(s, h, p, start, n, kind)

    def pick(p, i, pieces):
        chosen = pieces[0]
        for j in range(1, n_row):
            chosen = jnp.where(routes_ref[p, i] == j, pieces[j], chosen)
        return chosen

    def raise_tops(p, j, block):
        cols = pl.ds(j * piece, piece)
        best = tops[p, :, cols]
        for t in range(block.shape[0] // 16):
            best = jnp.maximum(best, jnp.abs(block[t * 16 : t * 16 + 16]))
        tops[p, :, cols] = best

    def prepare_head(h, start, n):
        @pl.loop(0, n // 16)
        def _(g):
            here = pl.ds(pl.multiple_of(h * depth + start + g * 16, 16), 16)
            pieces = [sent[j, here, :] for j in range(n_row)]
            for j in range(n_row):
                raise_tops(0, j, pieces[j])
            for i in range(n_row):
                sent[i, here, :] = pick(0, i, pieces)

    def scan(p, h, start, n, rows):
        @pl.loop(0, n // rows)
        def _(g):
            here = pl.ds(pl.multiple_of(p * height + h * depth + start + g * rows, 16), rows)
            for j in range(n_row):
                raise_tops(p, j, sent[j, here, :])

    def place(k):
        slot = k // ratio + 1
        return lax.rem(k, ratio), slot // slots, lax.rem(slot, slots) * size

    def prepare(k):
        h, p, start = place(k)
        src, _ = rows_of(h, p, start, size)

        @pl.loop(0, size // 16)
        def _(g):
            here = pl.ds(pl.multiple_of(src.start + g * 16, 16), 16)
            pieces = [sent[j, here, :] for j in range(n_row)]
            for i in range(n_row):
                value = pick(p, i, pieces).astype(jnp.float32)
                sent[i, here, :] = (value * factor[p * n_row + i]).astype(sent.dtype)

    def begin(k):
        h, p, start = place(k)
        start_first(len(heads) + k, h, p, start, size)
        start_second(0, h, p, start, size, 1)

    barrier = pltpu.get_barrier_semaphore()
    for s in range(1, n_row):
        pl.semaphore_signal(barrier, inc=1, device_id=(peer_row(s), col), device_id_type=MESH)
    for s in range(1, n_col):
        pl.semaphore_signal(barrier, inc=1, device_id=(row, peer_col(s)), device_id_type=MESH)

    for h in range(ratio):
        fetch(0, h, 0, size, h)
    blocks = [(p, h) for p in range(2) for h in range(ratio)]
    for b, (p, h) in enumerate(blocks):
        start = size if p == 0 else 0
        fetch(p, h, start, depth - start, ratio + b)
    tops[...] = jnp.zeros_like(tops)

    for h in range(ratio):
        fetched(0, h, 0, size, h)
    for h, q, n in heads:
        prepare_head(h, q, n)

    pl.semaphore_wait(barrier, n_row + n_col - 2)
    for e, (h, q, n) in enumerate(heads):
        start_first(e, h, 0, q, n)
        start_second(0, h, 0, q, n, 0)

    def scan_block(b):
        p, h = blocks[b]
        start = size if p == 0 else 0
        fetched(p, h, start, depth - start, ratio + b)
        scan(p, h, start, depth - start, size if size % 16 == 0 else 16)

    def forward_head(e):
        h, q, n = heads[e]
        forward(e, h, 0, q, n, 0)

    waiting = list(range(len(heads)))
    for b in range(len(blocks)):
        scan_block(b)
        if b >= 1 and waiting:
            forward_head(waiting.pop(0))

    for p in range(2):
        pieces = [
            jnp.max(tops[p, :, pl.ds(j * piece, piece)].astype(jnp.float32), axis=0, keepdims=True)
            for j in range(n_row)
        ]
        for i in range(n_row):
            peak[i, pl.ds(p, 1), :] = pick(p, i, pieces)

    forward_head(waiting.pop(0))

    def peak_first(s):
        return remote(peak, peak_mid.at[s - 1], psend1.at[s - 1], precv1.at[s - 1], peer_row(s), col)

    for s in range(1, n_row):
        peak_first(s).start()
    while waiting:
        forward_head(waiting.pop(0))
    for s in range(1, n_row):
        peak_first(s).wait()
    for i in range(n_row):
        top = peak[i]
        for s in range(1, n_row):
            top = jnp.maximum(top, peak_mid[s - 1, i])
        total[i] = top
        value = LIMIT / (top + EPSILON)
        for p in range(2):
            factor[p * n_row + i] = value[p : p + 1]

    def peak_second(s):
        return remote(
            total.at[row], peak_all.at[col], psend2.at[s - 1], precv2.at[col], row, peer_col(s)
        )

    prepare(0)
    for s in range(1, n_col):
        peak_second(s).start()
    peak_all[col] = total[row]

    @pl.loop(0, steps + LAG)
    def _(k):
        @pl.when(k + 1 < steps)
        def _():
            prepare(k + 1)

        @pl.when(k < steps)
        def _():
            begin(k)

        @pl.when(k >= LAG)
        def _():
            h, p, start = place(k - LAG)
            forward(len(heads) + k - LAG, h, p, start, size, 1)

    for s in range(1, n_col):
        peak_second(s).wait_send()
        other = peer_col(s)
        local(peak_all.at[other], peak_all.at[other], precv2.at[other]).wait()
        block = got_ref.at[other, pl.ds(0, size)]
        local(block, block, recv2.at[0, other]).wait()
    for c in range(n_col):
        base = peak_all[c] + EPSILON
        scales_ref[:, pl.ds(c * piece, piece)] = base / LIMIT
        value = (LIMIT / base)[0:1]

        @pl.loop(0, size // 16)
        def _(g):
            here = pl.ds(pl.multiple_of(g * 16, 16), 16)
            got_ref[c, here, :] = (got_ref[c, here, :].astype(jnp.float32) * value).astype(got_ref.dtype)

    for s in range(1, n_row):
        local(sent.at[0], sent.at[0], send1.at[s - 1]).wait()
    for s in range(n_row):
        kept = peer_row(n_row - s) == col // ratio

        @pl.when(kept)
        def _():
            part = sent.at[0, pl.ds(0, 2 * height - 2 * depth)]
            local(part, part, send2.at[s]).wait()

        @pl.when(jnp.logical_not(kept))
        def _():
            local(sent.at[0], sent.at[0], send2.at[s]).wait()

    for s in range(1, n_col):
        other = peer_col(s)
        block = got_ref.at[other, pl.ds(size, 2 * depth - size)]
        local(block, block, recv2.at[1, other]).wait()


def move_call(gate_weight, up_weight, routes, n_row, n_col, parts):
    height, width = gate_weight.shape
    kind = gate_weight.dtype
    piece = width // n_row
    ratio = n_col // n_row
    depth = height // ratio
    size = depth // parts
    head = [(0, 16), (16, 16), (32, size - 32)]
    copies = len(head) * ratio + (2 * parts - 1) * ratio
    dma = pltpu.SemaphoreType.DMA
    return pl.pallas_call(
        functools.partial(move_kernel, n_row, n_col, depth, size, head),
        out_shape=[
            pltpu.VMEM((n_col, 2 * depth, piece), kind),
            pltpu.VMEM((2, n_col * piece), jnp.float32),
        ],
        in_specs=[
            pl.BlockSpec(memory_space=pltpu.SMEM),
            pl.BlockSpec(memory_space=pl.ANY),
            pl.BlockSpec(memory_space=pl.ANY),
        ],
        out_specs=[
            pl.BlockSpec(memory_space=pltpu.VMEM),
            pl.BlockSpec(memory_space=pltpu.VMEM),
        ],
        scratch_shapes=[
            pltpu.VMEM((n_row, 2 * height, piece), kind),
            pltpu.VMEM((n_row - 1, 2 * height, piece), kind),
            pltpu.VMEM((2, 16, width), kind),
            pltpu.VMEM((n_row, 2, piece), jnp.float32),
            pltpu.VMEM((n_row - 1, n_row, 2, piece), jnp.float32),
            pltpu.VMEM((n_row, 2, piece), jnp.float32),
            pltpu.VMEM((2 * n_row, 1, piece), jnp.float32),
            pltpu.VMEM((n_col, 2, piece), jnp.float32),
            dma((3 * ratio,)),
            dma((n_row - 1,)),
            dma((copies, n_row - 1)),
            dma((n_row,)),
            dma((2, n_col)),
            dma((n_row - 1,)),
            dma((n_row - 1,)),
            dma((n_col - 1,)),
            dma((n_col,)),
        ],
        compiler_params=pltpu.CompilerParams(
            collective_id=0, has_side_effects=True, vmem_limit_bytes=MOVE_BYTES
        ),
    )(routes, gate_weight, up_weight)


def store_kernel(depth, piece, got_ref, scales_ref, gate_ref, up_ref, out_ref, sems):
    copies = [pltpu.make_async_copy(scales_ref, out_ref, sems.at[2 * got_ref.shape[0]])]
    for c in range(got_ref.shape[0]):
        for p, ref in enumerate((gate_ref, up_ref)):
            copies.append(
                pltpu.make_async_copy(
                    got_ref.at[c, pl.ds(p * depth, depth)],
                    ref.at[:, pl.ds(c * piece, piece)],
                    sems.at[2 * c + p],
                )
            )
    for copy in copies:
        copy.start()
    for copy in copies:
        copy.wait()


def store_call(got, scales):
    n_col, double, piece = got.shape
    depth = double // 2
    any_spec = pl.BlockSpec(memory_space=pl.ANY)
    return pl.pallas_call(
        functools.partial(store_kernel, depth, piece),
        in_specs=[pl.BlockSpec(memory_space=pltpu.VMEM), pl.BlockSpec(memory_space=pltpu.VMEM)],
        out_specs=[any_spec] * 3,
        out_shape=[
            jax.ShapeDtypeStruct((depth, n_col * piece), got.dtype),
            jax.ShapeDtypeStruct((depth, n_col * piece), got.dtype),
            jax.ShapeDtypeStruct((2, n_col * piece), jnp.float32),
        ],
        scratch_shapes=[pltpu.SemaphoreType.DMA((2 * n_col + 1,))],
        compiler_params=pltpu.CompilerParams(vmem_limit_bytes=STORE_BYTES),
    )(got, scales)


def kernel_shards(n_row, n_col, gate_weight, up_weight, routes):
    got, scales = move_call(gate_weight, up_weight, routes, n_row, n_col, PARTS)
    return tuple(store_call(got, scales))


def fits(n_row, n_col, height, width):
    if n_col % n_row or width % n_row or (width // n_row) % 128:
        return False
    ratio = n_col // n_row
    if height % (ratio * PARTS * 16) or height // (ratio * PARTS) < 48:
        return False
    held_bytes = ((2 * n_row - 1) * 2 * height + n_col * 2 * height // ratio) * (width // n_row) * 2
    return held_bytes < 60 * 1024 * 1024


def solution(mesh):
    n_row, n_col = mesh.shape["row"], mesh.shape["col"]

    def shards(gate_weight, up_weight, routes):
        if fits(n_row, n_col, *gate_weight.shape):
            return kernel_shards(n_row, n_col, gate_weight, up_weight, routes)
        return plain_shards(gate_weight, up_weight, routes)

    return jax.shard_map(
        shards,
        mesh=mesh,
        in_specs=(P("row", "col"), P("row", "col"), P()),
        out_specs=(P("col", "row"), P("col", "row"), P(None, "row")),
        check_vma=False,
    )
```

time: 497 us -> 477 us (0.960)
  Pallas kernels: 493 us -> 476 us
    pallas_call x2, Pallas kernels: 493 us -> 476 us  [the longest x1 469 us: move_call(): pl.pallas_call(functools.partial(move_kernel, n_row, n_col, depth, size,...]
where the time goes in v1:
time: 477 us
  Pallas kernels  476 us (100%)
    pallas_call x1, Pallas kernels, move_call(): pl.pallas_call(functools.partial(move_kernel, n_row, n_col, depth, size,...  469 us

profile of v1, /device:TPU:5, one launch (start us, length us, event | category | flops | bytes accessed | tf_op | source)
XLA Modules:
  0.0 476.6 jit_solution(14199680682828475602)
XLA Ops:
  0.6 468.6 %shard_map.58 = (bf16[8,1152,1152]{2,1,0:T(8,128)(2,1)S(1)}, f32[2,9216]{1,0:T(2,128)S(1)}) custom-call(s32[2,4]{1,0:T(2,128)} %routes_ref.1, bf16[1152,4608]{1,0:T(8,128)(2,1)} %gate_ref.1, bf16[1152,4608]{1,0:T(8,128)(2,1)} %up_ref.1), custom_call_target="tpu_custom_call" | custom-call | tf_op jit(solution)/shard_map/pallas_call | solution.py:340
  469.2 7.4 %shard_map.59 = (bf16[576,9216]{1,0:T(8,128)(2,1)}, bf16[576,9216]{1,0:T(8,128)(2,1)}, f32[2,9216]{1,0:T(2,128)}) custom-call(bf16[8,1152,1152]{2,1,0:T(8,128)(2,1)S(1)} %get-tuple-element.5.got_ref, f32[2,9216]{1,0:T(2,128)S(1)} %get-tuple-element.6.scales_ref), custom_call_target="tpu_custom_call" | custom-call | tf_op jit(solution)/shard_map/pallas_call | solution.py:401

commit v2 on v1

v2 whole, which is shorter than its diff:
```python
import functools

import jax
import jax.numpy as jnp
from jax import lax
from jax.experimental import pallas as pl
from jax.experimental.pallas import tpu as pltpu
from jax.sharding import PartitionSpec as P

EPSILON = 1e-06
LIMIT = 4.0
MESH = pl.DeviceIdType.MESH
MOVE_BYTES = 40 * 1024 * 1024
STORE_BYTES = 1024 * 1024
RAW = 64
SMALL = 4
LARGE = 4
LAG = 2


def column_peaks(weight):
    return jnp.max(jnp.abs(weight), axis=0).astype(jnp.float32)


def quantize(weight, peaks):
    factor = LIMIT / (peaks + EPSILON)
    return (weight.astype(jnp.float32) * factor[None, :]).astype(jnp.bfloat16)


def order_pieces(weight, order, pieces):
    height, width = weight.shape
    shaped = weight.reshape(height, pieces, width // pieces)
    return jnp.take(shaped, order, axis=1).reshape(height, width)


def own_piece(peaks, pick, pieces):
    shaped = ((peaks + EPSILON) / LIMIT).reshape(pieces, -1)
    return lax.dynamic_index_in_dim(shaped, pick, 0, keepdims=False)


def exchange(sent):
    sent = lax.all_to_all(sent, "row", split_axis=1, concat_axis=0, tiled=True)
    return lax.all_to_all(sent, "col", split_axis=0, concat_axis=1, tiled=True)


def plain_shards(gate_weight, up_weight, routes):
    pieces = lax.axis_size("row")
    row_index = lax.axis_index("row")
    gate_peaks, up_peaks = lax.pmax((column_peaks(gate_weight), column_peaks(up_weight)), "row")
    gate_serving = exchange(order_pieces(quantize(gate_weight, gate_peaks), routes[0], pieces))
    up_serving = exchange(order_pieces(quantize(up_weight, up_peaks), routes[1], pieces))
    chosen = jnp.take(routes, row_index, axis=1)
    local_scales = jnp.stack(
        [own_piece(gate_peaks, chosen[0], pieces), own_piece(up_peaks, chosen[1], pieces)]
    )
    scales = lax.all_gather(local_scales, "col", axis=1, tiled=True)
    return (gate_serving, up_serving, scales)


def move_kernel(
    n_row, n_col, depth, raw, head, bodies,
    routes_ref, gate_ref, up_ref, got_ref, scales_ref,
    routes, sent, mid, tops, peak, peak_mid, total, factor, peak_all,
    route_load, load, send1, head1, body1, send2, recv2, peak_send, peak_recv,
):
    row, col = lax.axis_index("row"), lax.axis_index("col")
    ratio = n_col // n_row
    height = ratio * depth
    piece = sent.shape[2]
    heads = [(h, q, n) for q, n in head for h in range(ratio)]
    mine = row * ratio

    def peer_row(s):
        return lax.rem(row + s, n_row)

    def peer_col(s):
        return lax.rem(col + s, n_col)

    def local(ref, target, sem):
        return pltpu.make_async_copy(ref, target, sem)

    def wait_bytes(ref, sem):
        local(ref, ref, sem).wait()

    def remote(ref, target, send, recv, to_row, to_col):
        return pltpu.make_async_remote_copy(
            src_ref=ref, dst_ref=target, send_sem=send, recv_sem=recv,
            device_id=(to_row, to_col), device_id_type=MESH,
        )

    def fetch(p, h, start, n, index):
        ref = (gate_ref, up_ref)[p]
        for j in range(n_row):
            local(
                ref.at[pl.ds(h * depth + start, n), pl.ds(j * piece, piece)],
                sent.at[j, pl.ds(p * height + h * depth + start, n)],
                load.at[index],
            ).start()

    def fetched(p, h, start, n, index):
        wait_bytes(sent.at[:, pl.ds(p * height + h * depth + start, n)], load.at[index])

    def rows_of(h, p, start, n):
        src = pl.ds(pl.multiple_of((p * ratio + h) * depth + start, 16), n)
        dst = pl.ds(pl.multiple_of(p * depth + start, 16), n)
        return src, dst

    def start_first(sems, h, p, start, n):
        src, dst = rows_of(h, p, start, n)
        for s in range(1, n_row):
            to = peer_row(s)

            @pl.when(mine + h != col)
            def _():
                remote(sent.at[to, src], mid.at[n_row - 1 - s, src], send1, sems[s - 1], to, col).start()

            @pl.when(mine + h == col)
            def _():
                remote(sent.at[to, src], got_ref.at[col, dst], send1, sems[s - 1], to, col).start()

    def start_second(s, h, p, start, n, kind):
        src, dst = rows_of(h, p, start, n)
        to = peer_row(n_row - s) * ratio + h
        block = sent.at[row, src] if s == 0 else mid.at[n_row - 1 - s, src]

        @pl.when(to != col)
        def _():
            remote(block, got_ref.at[col, dst], send2, recv2.at[kind], row, to).start()

        if s == 0:
            @pl.when(to == col)
            def _():
                @pl.loop(0, n // 16)
                def _(g):
                    here = pl.ds(pl.multiple_of(src.start + g * 16, 16), 16)
                    there = pl.ds(pl.multiple_of(dst.start + g * 16, 16), 16)
                    got_ref[col, there, :] = sent[row, here, :]

    def pick(p, i, pieces):
        chosen = pieces[0]
        for j in range(1, n_row):
            chosen = jnp.where(routes[p, i] == j, pieces[j], chosen)
        return chosen

    def raise_tops(p, j, block):
        cols = pl.ds(j * piece, piece)
        best = tops[p, :, cols]
        for t in range(block.shape[0] // 16):
            best = jnp.maximum(best, jnp.abs(block[t * 16 : t * 16 + 16]))
        tops[p, :, cols] = best

    def prepare_head(h, start, n):
        @pl.loop(0, n // 16)
        def _(g):
            here = pl.ds(pl.multiple_of(h * depth + start + g * 16, 16), 16)
            pieces = [sent[j, here, :] for j in range(n_row)]
            for j in range(n_row):
                raise_tops(0, j, pieces[j])
            for i in range(n_row):
                sent[i, here, :] = pick(0, i, pieces)

    blocks = [(p, h) for p in range(2) for h in range(ratio)]

    def block_start(p):
        return raw if p == 0 else 0

    def scan_block(b):
        p, h = blocks[b]
        start = block_start(p)
        n = depth - start
        fetched(p, h, start, n, 2 * ratio + b)

        @pl.loop(0, n // 64)
        def _(g):
            here = pl.ds(pl.multiple_of(p * height + h * depth + start + g * 64, 16), 64)
            for j in range(n_row):
                raise_tops(p, j, sent[j, here, :])

    def head_sems(e):
        return [head1.at[e, s] for s in range(n_row - 1)]

    def begin_head(e):
        h, q, n = heads[e]
        start_first(head_sems(e), h, 0, q, n)
        start_second(0, h, 0, q, n, 0)

    def forward_head(e):
        h, q, n = heads[e]
        src, _ = rows_of(h, 0, q, n)
        for s in range(1, n_row):
            wait_bytes(mid.at[n_row - 1 - s, src], head1.at[e, s - 1])
            start_second(s, h, 0, q, n, 0)

    barrier = pltpu.get_barrier_semaphore()
    for s in sorted(range(1, n_col), key=lambda s: -min(s, n_col - s)):
        pl.semaphore_signal(barrier, inc=1, device_id=(row, peer_col(s)), device_id_type=MESH)
    for s in range(1, n_row):
        pl.semaphore_signal(barrier, inc=1, device_id=(peer_row(s), col), device_id_type=MESH)

    route_copy = local(routes_ref, routes, route_load)
    route_copy.start()
    first = head[0][1]
    for h in range(ratio):
        fetch(0, h, 0, first, h)
    for h in range(ratio):
        fetch(0, h, first, raw - first, ratio + h)
    for b, (p, h) in enumerate(blocks):
        start = block_start(p)
        fetch(p, h, start, depth - start, 2 * ratio + b)
    tops[...] = jnp.zeros_like(tops)

    route_copy.wait()
    for h in range(ratio):
        fetched(0, h, 0, first, h)
    for e in range(ratio):
        prepare_head(*heads[e])
    for h in range(ratio):
        fetched(0, h, first, raw - first, ratio + h)
    for e in range(ratio, len(heads)):
        prepare_head(*heads[e])
    scan_block(0)

    held = len(heads) - ratio
    pl.semaphore_wait(barrier, n_row + n_col - 2)
    for e in range(held):
        begin_head(e)
    scan_block(1)
    forward_head(0)
    scan_block(2)
    forward_head(1)
    for b in range(3, len(blocks)):
        scan_block(b)

    for p in range(2):
        pieces = [
            jnp.max(tops[p, :, pl.ds(j * piece, piece)].astype(jnp.float32), axis=0, keepdims=True)
            for j in range(n_row)
        ]
        for i in range(n_row):
            peak[i, pl.ds(p, 1), :] = pick(p, i, pieces)

    forward_head(2)
    for s in range(1, n_row):
        remote(peak, peak_mid.at[s - 1], peak_send.at[0], peak_recv.at[0], peer_row(s), col).start()
    for e in range(held, len(heads)):
        begin_head(e)
    for e in range(3, held):
        forward_head(e)

    wait_bytes(peak_mid, peak_recv.at[0])
    for i in range(n_row):
        top = peak[i]
        for s in range(1, n_row):
            top = jnp.maximum(top, peak_mid[s - 1, i])
        total[i] = top
        value = LIMIT / (top + EPSILON)
        for p in range(2):
            factor[p * n_row + i] = value[p : p + 1]

    late = list(range(held, len(heads)))
    base = 0
    for p, (start, size, count) in enumerate(bodies):
        def place(k, start=start, size=size):
            return lax.rem(k, ratio), start + (k // ratio) * size

        def prepare(k, p=p, size=size, place=place):
            h, at = place(k)
            src, _ = rows_of(h, p, at, size)

            @pl.loop(0, size // 16)
            def _(g):
                here = pl.ds(pl.multiple_of(src.start + g * 16, 16), 16)
                pieces = [sent[j, here, :] for j in range(n_row)]
                for i in range(n_row):
                    value = pick(p, i, pieces).astype(jnp.float32)
                    sent[i, here, :] = (value * factor[p * n_row + i]).astype(sent.dtype)

        def begin(k, p=p, size=size, base=base, place=place):
            h, at = place(k)
            start_first([body1.at[base + k]] * (n_row - 1), h, p, at, size)
            start_second(0, h, p, at, size, 1)

        def forward(k, p=p, size=size, base=base, place=place):
            h, at = place(k)
            src, _ = rows_of(h, p, at, size)
            wait_bytes(mid.at[:, src], body1.at[base + k])
            for s in range(1, n_row):
                start_second(s, h, p, at, size, 1)

        steps = count * ratio
        prepare(0)
        if p == 0:
            for s in range(1, n_col):
                remote(
                    total.at[row], peak_all.at[col], peak_send.at[1], peak_recv.at[1], row, peer_col(s)
                ).start()
            peak_all[col] = total[row]
        prepare(1)
        begin(0)
        for e in late:
            forward_head(e)
        late = []

        @pl.loop(1, steps + LAG)
        def _(k, steps=steps, prepare=prepare, begin=begin, forward=forward):
            @pl.when(k + 1 < steps)
            def _():
                prepare(k + 1)

            @pl.when(k < steps)
            def _():
                begin(k)

            @pl.when(k >= LAG)
            def _():
                forward(k - LAG)

        base += steps

    others = pl.ds(0, n_col - 1)
    wait_bytes(peak_all.at[others], peak_send.at[1])
    wait_bytes(peak_all.at[others], peak_recv.at[1])
    wait_bytes(got_ref.at[others, pl.ds(0, raw)], recv2.at[0])
    for c in range(n_col):
        base_peak = peak_all[c] + EPSILON
        scales_ref[:, pl.ds(c * piece, piece)] = base_peak / LIMIT
        value = (LIMIT / base_peak)[0:1]

        @pl.loop(0, raw // 16)
        def _(g):
            here = pl.ds(pl.multiple_of(g * 16, 16), 16)
            got_ref[c, here, :] = (got_ref[c, here, :].astype(jnp.float32) * value).astype(got_ref.dtype)

    wait_bytes(peak_mid, peak_send.at[0])
    wait_bytes(mid, send1)
    wait_bytes(got_ref.at[others], send2)
    wait_bytes(got_ref.at[others, pl.ds(raw, 2 * depth - raw)], recv2.at[1])


def move_call(gate_weight, up_weight, routes, n_row, n_col):
    height, width = gate_weight.shape
    kind = gate_weight.dtype
    piece = width // n_row
    ratio = n_col // n_row
    depth = height // ratio
    head = [(0, 16), (16, 16), (32, RAW - 32)]
    small = SMALL * 16
    large = depth // LARGE
    bodies = [(RAW, small, (depth - RAW) // small), (0, large, LARGE)]
    steps = sum(count for _, _, count in bodies) * ratio
    dma = pltpu.SemaphoreType.DMA
    return pl.pallas_call(
        functools.partial(move_kernel, n_row, n_col, depth, RAW, head, bodies),
        out_shape=[
            pltpu.VMEM((n_col, 2 * depth, piece), kind),
            pltpu.VMEM((2, n_col * piece), jnp.float32),
        ],
        in_specs=[pl.BlockSpec(memory_space=pl.ANY)] * 3,
        out_specs=[
            pl.BlockSpec(memory_space=pltpu.VMEM),
            pl.BlockSpec(memory_space=pltpu.VMEM),
        ],
        scratch_shapes=[
            pltpu.SMEM(routes.shape, routes.dtype),
            pltpu.VMEM((n_row, 2 * height, piece), kind),
            pltpu.VMEM((n_row - 1, 2 * height, piece), kind),
            pltpu.VMEM((2, 16, width), kind),
            pltpu.VMEM((n_row, 2, piece), jnp.float32),
            pltpu.VMEM((n_row - 1, n_row, 2, piece), jnp.float32),
            pltpu.VMEM((n_row, 2, piece), jnp.float32),
            pltpu.VMEM((2 * n_row, 1, piece), jnp.float32),
            pltpu.VMEM((n_col, 2, piece), jnp.float32),
            dma,
            dma((4 * ratio,)),
            dma,
            dma((len(head) * ratio, n_row - 1)),
            dma((steps,)),
            dma,
            dma((2,)),
            dma((2,)),
            dma((2,)),
        ],
        compiler_params=pltpu.CompilerParams(
            collective_id=0, has_side_effects=True, vmem_limit_bytes=MOVE_BYTES
        ),
    )(routes, gate_weight, up_weight)


def store_kernel(depth, piece, got_ref, scales_ref, gate_ref, up_ref, out_ref, sems):
    copies = [pltpu.make_async_copy(scales_ref, out_ref, sems.at[2 * got_ref.shape[0]])]
    for c in range(got_ref.shape[0]):
        for p, ref in enumerate((gate_ref, up_ref)):
            copies.append(
                pltpu.make_async_copy(
                    got_ref.at[c, pl.ds(p * depth, depth)],
                    ref.at[:, pl.ds(c * piece, piece)],
                    sems.at[2 * c + p],
                )
            )
    for copy in copies:
        copy.start()
    for copy in copies:
        copy.wait()


def store_call(got, scales):
    n_col, double, piece = got.shape
    depth = double // 2
    any_spec = pl.BlockSpec(memory_space=pl.ANY)
    return pl.pallas_call(
        functools.partial(store_kernel, depth, piece),
        in_specs=[pl.BlockSpec(memory_space=pltpu.VMEM), pl.BlockSpec(memory_space=pltpu.VMEM)],
        out_specs=[any_spec] * 3,
        out_shape=[
            jax.ShapeDtypeStruct((depth, n_col * piece), got.dtype),
            jax.ShapeDtypeStruct((depth, n_col * piece), got.dtype),
            jax.ShapeDtypeStruct((2, n_col * piece), jnp.float32),
        ],
        scratch_shapes=[pltpu.SemaphoreType.DMA((2 * n_col + 1,))],
        compiler_params=pltpu.CompilerParams(vmem_limit_bytes=STORE_BYTES),
    )(got, scales)


def kernel_shards(n_row, n_col, gate_weight, up_weight, routes):
    got, scales = move_call(gate_weight, up_weight, routes, n_row, n_col)
    return tuple(store_call(got, scales))


def fits(n_row, n_col, height, width):
    if n_col % n_row or width % n_row or (width // n_row) % 128:
        return False
    ratio = n_col // n_row
    depth = height // ratio
    if ratio != 2 or height % ratio or depth % (LARGE * 16) or depth % 64 or (depth - RAW) % (SMALL * 16):
        return False
    held_bytes = ((2 * n_row - 1) * 2 * height + n_col * 2 * height // ratio) * (width // n_row) * 2
    return held_bytes < 60 * 1024 * 1024


def solution(mesh):
    n_row, n_col = mesh.shape["row"], mesh.shape["col"]

    def shards(gate_weight, up_weight, routes):
        if fits(n_row, n_col, *gate_weight.shape):
            return kernel_shards(n_row, n_col, gate_weight, up_weight, routes)
        return plain_shards(gate_weight, up_weight, routes)

    return jax.shard_map(
        shards,
        mesh=mesh,
        in_specs=(P("row", "col"), P("row", "col"), P()),
        out_specs=(P("col", "row"), P("col", "row"), P(None, "row")),
        check_vma=False,
    )
```

time: 477 us -> 475 us (level)
  no operation moved by 1% of the time
where the time goes in v2:
time: 475 us
  Pallas kernels  474 us (100%)
    pallas_call x1, Pallas kernels, move_call(): pl.pallas_call(functools.partial(move_kernel, n_row, n_col, depth, RAW, h...  467 us

profile of v2, /device:TPU:5, one launch (start us, length us, event | category | flops | bytes accessed | tf_op | source)
XLA Modules:
  0.0 474.9 jit_solution(10448462290853419738)
XLA Ops:
  0.6 466.9 %shard_map.58 = (bf16[8,1152,1152]{2,1,0:T(8,128)(2,1)S(1)}, f32[2,9216]{1,0:T(2,128)S(1)}) custom-call(s32[2,4]{1,0:T(2,128)} %routes_ref.1, bf16[1152,4608]{1,0:T(8,128)(2,1)} %gate_ref.1, bf16[1152,4608]{1,0:T(8,128)(2,1)} %up_ref.1), custom_call_target="tpu_custom_call" | custom-call | tf_op jit(solution)/shard_map/pallas_call | solution.py:352
  467.6 7.4 %shard_map.59 = (bf16[576,9216]{1,0:T(8,128)(2,1)}, bf16[576,9216]{1,0:T(8,128)(2,1)}, f32[2,9216]{1,0:T(2,128)}) custom-call(bf16[8,1152,1152]{2,1,0:T(8,128)(2,1)S(1)} %get-tuple-element.5.got_ref, f32[2,9216]{1,0:T(2,128)S(1)} %get-tuple-element.6.scales_ref), custom_call_target="tpu_custom_call" | custom-call | tf_op jit(solution)/shard_map/pallas_call | solution.py:410

commit v3 on v2

--- a/solution.py
+++ b/solution.py
@@ -14,7 +14,8 @@
 STORE_BYTES = 1024 * 1024
 RAW = 64
 SMALL = 4
-LARGE = 4
+LARGE = 5
+MINI = 16
 LAG = 2
 
 
@@ -58,10 +59,10 @@
 
 
 def move_kernel(
-    n_row, n_col, depth, raw, head, bodies,
+    n_row, n_col, depth, raw, head, mini, bodies,
     routes_ref, gate_ref, up_ref, got_ref, scales_ref,
-    routes, sent, mid, tops, peak, peak_mid, total, factor, peak_all,
-    route_load, load, send1, head1, body1, send2, recv2, peak_send, peak_recv,
+    routes, sent, mid, relay, tops, peak, peak_mid, total, factor, peak_all,
+    route_load, load, send1, head1, mini1, body1, send2, recv2, peak_send, peak_recv, relay_sems,
 ):
     row, col = lax.axis_index("row"), lax.axis_index("col")
     ratio = n_col // n_row
@@ -69,6 +70,11 @@
     piece = sent.shape[2]
     heads = [(h, q, n) for q, n in head for h in range(ratio)]
     mine = row * ratio
+
+    half = n_row // 2
+    near = [half] + [half + t * (1 - 2 * (row % 2)) for u in range(1, half) for t in (u, -u)]
+    close = [half] + [half - t * (1 - 2 * (row % 2)) for u in range(1, half) for t in (u, -u)]
+    far = [s + (row // half) * (n_row - 2 * s) for s in range(1, n_row)]
 
     def peer_row(s):
         return lax.rem(row + s, n_row)
@@ -107,27 +113,28 @@
 
     def start_first(sems, h, p, start, n):
         src, dst = rows_of(h, p, start, n)
-        for s in range(1, n_row):
+        for s in near:
             to = peer_row(s)
 
             @pl.when(mine + h != col)
             def _():
-                remote(sent.at[to, src], mid.at[n_row - 1 - s, src], send1, sems[s - 1], to, col).start()
+                remote(sent.at[to, src], mid.at[n_row - 1 - s, src], send1, sems(s), to, col).start()
 
             @pl.when(mine + h == col)
             def _():
-                remote(sent.at[to, src], got_ref.at[col, dst], send1, sems[s - 1], to, col).start()
-
-    def start_second(s, h, p, start, n, kind):
+                remote(sent.at[to, src], got_ref.at[col, dst], send1, sems(s), to, col).start()
+
+    def start_second(s, h, p, start, n, kind, send=0):
         src, dst = rows_of(h, p, start, n)
         to = peer_row(n_row - s) * ratio + h
-        block = sent.at[row, src] if s == 0 else mid.at[n_row - 1 - s, src]
+        own = isinstance(s, int) and s == 0
+        block = sent.at[row, src] if own else mid.at[n_row - 1 - s, src]
 
         @pl.when(to != col)
         def _():
-            remote(block, got_ref.at[col, dst], send2, recv2.at[kind], row, to).start()
-
-        if s == 0:
+            remote(block, got_ref.at[col, dst], send2.at[send], recv2.at[kind], row, to).start()
+
+        if own:
             @pl.when(to == col)
             def _():
                 @pl.loop(0, n // 16)
@@ -177,7 +184,7 @@
                 raise_tops(p, j, sent[j, here, :])
 
     def head_sems(e):
-        return [head1.at[e, s] for s in range(n_row - 1)]
+        return lambda s: head1.at[e, s - 1]
 
     def begin_head(e):
         h, q, n = heads[e]
@@ -187,7 +194,7 @@
     def forward_head(e):
         h, q, n = heads[e]
         src, _ = rows_of(h, 0, q, n)
-        for s in range(1, n_row):
+        for s in close:
             wait_bytes(mid.at[n_row - 1 - s, src], head1.at[e, s - 1])
             start_second(s, h, 0, q, n, 0)
 
@@ -218,16 +225,15 @@
         fetched(0, h, first, raw - first, ratio + h)
     for e in range(ratio, len(heads)):
         prepare_head(*heads[e])
-    scan_block(0)
-
     held = len(heads) - ratio
     pl.semaphore_wait(barrier, n_row + n_col - 2)
     for e in range(held):
         begin_head(e)
+    scan_block(0)
+    forward_head(0)
+    forward_head(1)
     scan_block(1)
-    forward_head(0)
     scan_block(2)
-    forward_head(1)
     for b in range(3, len(blocks)):
         scan_block(b)
 
@@ -257,6 +263,48 @@
         for p in range(2):
             factor[p * n_row + i] = value[p : p + 1]
 
+    def prepare_rows(h, p, start, n):
+        src, _ = rows_of(h, p, start, n)
+
+        @pl.loop(0, n // 16)
+        def _(g):
+            here = pl.ds(pl.multiple_of(src.start + g * 16, 16), 16)
+            pieces = [sent[j, here, :] for j in range(n_row)]
+            for i in range(n_row):
+                value = pick(p, i, pieces).astype(jnp.float32)
+                sent[i, here, :] = (value * factor[p * n_row + i]).astype(sent.dtype)
+
+    back = peer_row(n_row - half) * ratio
+
+    def begin_mini(h):
+        src, dst = rows_of(h, 1, 0, mini)
+        for t, s in enumerate(near):
+            to = peer_row(s)
+
+            @pl.when(mine + h == col)
+            def _():
+                remote(sent.at[to, src], got_ref.at[col, dst], send1, mini1.at[h, s - 1], to, col).start()
+
+            @pl.when(mine + h != col)
+            def _():
+                if h == 0 and t == 0:
+                    remote(sent.at[to, src], relay.at[col], send1, relay_sems.at[0], row, mine).start()
+                else:
+                    remote(sent.at[to, src], mid.at[n_row - 1 - s, src], send1, mini1.at[h, s - 1], to, col).start()
+        start_second(0, h, 1, 0, mini, 1, 1)
+
+    def forward_mini(h):
+        src, _ = rows_of(h, 1, 0, mini)
+        for t, s in enumerate(close):
+            block = mid.at[n_row - 1 - s, src]
+            if h == 0 and t == 0:
+                @pl.when(back == col)
+                def _():
+                    wait_bytes(block, mini1.at[h, s - 1])
+            else:
+                wait_bytes(block, mini1.at[h, s - 1])
+                start_second(s, h, 1, 0, mini, 1, 1)
+
     late = list(range(held, len(heads)))
     base = 0
     for p, (start, size, count) in enumerate(bodies):
@@ -265,31 +313,28 @@
 
         def prepare(k, p=p, size=size, place=place):
             h, at = place(k)
-            src, _ = rows_of(h, p, at, size)
-
-            @pl.loop(0, size // 16)
-            def _(g):
-                here = pl.ds(pl.multiple_of(src.start + g * 16, 16), 16)
-                pieces = [sent[j, here, :] for j in range(n_row)]
-                for i in range(n_row):
-                    value = pick(p, i, pieces).astype(jnp.float32)
-                    sent[i, here, :] = (value * factor[p * n_row + i]).astype(sent.dtype)
+            prepare_rows(h, p, at, size)
 
         def begin(k, p=p, size=size, base=base, place=place):
             h, at = place(k)
-            start_first([body1.at[base + k]] * (n_row - 1), h, p, at, size)
+            start_first(lambda s: body1.at[base + k], h, p, at, size)
             start_second(0, h, p, at, size, 1)
 
         def forward(k, p=p, size=size, base=base, place=place):
             h, at = place(k)
             src, _ = rows_of(h, p, at, size)
             wait_bytes(mid.at[:, src], body1.at[base + k])
-            for s in range(1, n_row):
+            for s in far:
                 start_second(s, h, p, at, size, 1)
 
         steps = count * ratio
+        if p == 0:
+            for h in range(ratio):
+                prepare_rows(h, 1, 0, mini)
         prepare(0)
         if p == 0:
+            for h in range(ratio):
+                begin_mini(h)
             for s in range(1, n_col):
                 remote(
                     total.at[row], peak_all.at[col], peak_send.at[1], peak_recv.at[1], row, peer_col(s)
@@ -299,6 +344,9 @@
         begin(0)
         for e in late:
             forward_head(e)
+        if p == 0:
+            for h in range(ratio):
+                forward_mini(h)
         late = []
 
         @pl.loop(1, steps + LAG)
@@ -318,6 +366,17 @@
         base += steps
 
     others = pl.ds(0, n_col - 1)
+
+    @pl.when(mine == col)
+    def _():
+        wait_bytes(relay.at[others], relay_sems.at[0])
+        _, dst = rows_of(0, 1, 0, mini)
+        for s in range(1, n_col):
+            other = peer_col(s)
+            remote(
+                relay.at[other], got_ref.at[other, dst], relay_sems.at[1], recv2.at[1], peer_row(half), col
+            ).start()
+
     wait_bytes(peak_all.at[others], peak_send.at[1])
     wait_bytes(peak_all.at[others], peak_recv.at[1])
     wait_bytes(got_ref.at[others, pl.ds(0, raw)], recv2.at[0])
@@ -333,7 +392,20 @@
 
     wait_bytes(peak_mid, peak_send.at[0])
     wait_bytes(mid, send1)
-    wait_bytes(got_ref.at[others], send2)
+    wait_bytes(got_ref.at[others, pl.ds(0, 2 * depth - mini)], send2.at[0])
+
+    @pl.when(back == col)
+    def _():
+        wait_bytes(sent.at[0, pl.ds(0, (n_row * ratio - 1) * mini)], send2.at[1])
+
+    @pl.when(back != col)
+    def _():
+        wait_bytes(sent.at[0, pl.ds(0, (n_row * ratio - 2) * mini)], send2.at[1])
+
+    @pl.when(mine == col)
+    def _():
+        wait_bytes(relay.at[others], relay_sems.at[1])
+
     wait_bytes(got_ref.at[others, pl.ds(raw, 2 * depth - raw)], recv2.at[1])
 
 
@@ -343,14 +415,14 @@
     piece = width // n_row
     ratio = n_col // n_row
     depth = height // ratio
-    head = [(0, 16), (16, 16), (32, RAW - 32)]
+    head = [(q, 16) for q in range(0, RAW, 16)]
     small = SMALL * 16
-    large = depth // LARGE
-    bodies = [(RAW, small, (depth - RAW) // small), (0, large, LARGE)]
+    large = (depth - MINI) // LARGE
+    bodies = [(RAW, small, (depth - RAW) // small), (MINI, large, LARGE)]
     steps = sum(count for _, _, count in bodies) * ratio
     dma = pltpu.SemaphoreType.DMA
     return pl.pallas_call(
-        functools.partial(move_kernel, n_row, n_col, depth, RAW, head, bodies),
+        functools.partial(move_kernel, n_row, n_col, depth, RAW, head, MINI, bodies),
         out_shape=[
             pltpu.VMEM((n_col, 2 * depth, piece), kind),
             pltpu.VMEM((2, n_col * piece), jnp.float32),
@@ -364,6 +436,7 @@
             pltpu.SMEM(routes.shape, routes.dtype),
             pltpu.VMEM((n_row, 2 * height, piece), kind),
             pltpu.VMEM((n_row - 1, 2 * height, piece), kind),
+            pltpu.VMEM((n_col, MINI, piece), kind),
             pltpu.VMEM((2, 16, width), kind),
             pltpu.VMEM((n_row, 2, piece), jnp.float32),
             pltpu.VMEM((n_row - 1, n_row, 2, piece), jnp.float32),
@@ -374,8 +447,10 @@
             dma((4 * ratio,)),
             dma,
             dma((len(head) * ratio, n_row - 1)),
+            dma((ratio, n_row - 1)),
             dma((steps,)),
-            dma,
+            dma((2,)),
+            dma((2,)),
             dma((2,)),
             dma((2,)),
             dma((2,)),
@@ -387,20 +462,14 @@
 
 
 def store_kernel(depth, piece, got_ref, scales_ref, gate_ref, up_ref, out_ref, sems):
-    copies = [pltpu.make_async_copy(scales_ref, out_ref, sems.at[2 * got_ref.shape[0]])]
     for c in range(got_ref.shape[0]):
         for p, ref in enumerate((gate_ref, up_ref)):
-            copies.append(
-                pltpu.make_async_copy(
-                    got_ref.at[c, pl.ds(p * depth, depth)],
-                    ref.at[:, pl.ds(c * piece, piece)],
-                    sems.at[2 * c + p],
-                )
-            )
-    for copy in copies:
-        copy.start()
-    for copy in copies:
-        copy.wait()
+            block = got_ref.at[c, pl.ds(p * depth, depth)]
+            pltpu.make_async_copy(block, ref.at[:, pl.ds(c * piece, piece)], sems.at[0]).start()
+    scales = pltpu.make_async_copy(scales_ref, out_ref, sems.at[1])
+    scales.start()
+    pltpu.make_async_copy(got_ref, got_ref, sems.at[0]).wait()
+    scales.wait()
 
 
 def store_call(got, scales):
@@ -416,7 +485,7 @@
             jax.ShapeDtypeStruct((depth, n_col * piece), got.dtype),
             jax.ShapeDtypeStruct((2, n_col * piece), jnp.float32),
         ],
-        scratch_shapes=[pltpu.SemaphoreType.DMA((2 * n_col + 1,))],
+        scratch_shapes=[pltpu.SemaphoreType.DMA((2,))],
         compiler_params=pltpu.CompilerParams(vmem_limit_bytes=STORE_BYTES),
     )(got, scales)
 
@@ -431,7 +500,7 @@
         return False
     ratio = n_col // n_row
     depth = height // ratio
-    if ratio != 2 or height % ratio or depth % (LARGE * 16) or depth % 64 or (depth - RAW) % (SMALL * 16):
+    if ratio != 2 or n_row != 4 or height % ratio or (depth - MINI) % (LARGE * 16) or depth % 64 or (depth - RAW) % (SMALL * 16):
         return False
     held_bytes = ((2 * n_row - 1) * 2 * height + n_col * 2 * height // ratio) * (width // n_row) * 2
     return held_bytes < 60 * 1024 * 1024

time: 475 us -> 473 us (level); the launches traced: 475 us -> 468 us
  Pallas kernels: 474 us -> 467 us
    pallas_call x1, Pallas kernels: 467 us -> 460 us  [move_call(): pl.pallas_call(functools.partial(move_kernel, n_row, n_col, depth, RAW, h...]
where the time goes in v3:
time: 473 us; the launch traced here: 468 us
  Pallas kernels  467 us (99%)
    pallas_call x1, Pallas kernels, move_call(): pl.pallas_call(functools.partial(move_kernel, n_row, n_col, depth, RAW, h...  460 us

profile of v3, /device:TPU:5, one launch (start us, length us, event | category | flops | bytes accessed | tf_op | source)
XLA Modules:
  0.0 467.9 jit_solution(313093165376311920)
XLA Ops:
  0.6 460.0 %shard_map.58 = (bf16[8,1152,1152]{2,1,0:T(8,128)(2,1)S(1)}, f32[2,9216]{1,0:T(2,128)S(1)}) custom-call(s32[2,4]{1,0:T(2,128)} %routes_ref.1, bf16[1152,4608]{1,0:T(8,128)(2,1)} %gate_ref.1, bf16[1152,4608]{1,0:T(8,128)(2,1)} %up_ref.1), custom_call_target="tpu_custom_call" | custom-call | tf_op jit(solution)/shard_map/pallas_call | solution.py:424
  460.7 7.2 %shard_map.59 = (bf16[576,9216]{1,0:T(8,128)(2,1)}, bf16[576,9216]{1,0:T(8,128)(2,1)}, f32[2,9216]{1,0:T(2,128)}) custom-call(bf16[8,1152,1152]{2,1,0:T(8,128)(2,1)S(1)} %get-tuple-element.5.got_ref, f32[2,9216]{1,0:T(2,128)S(1)} %get-tuple-element.6.scales_ref), custom_call_target="tpu_custom_call" | custom-call | tf_op jit(solution)/shard_map/pallas_call | solution.py:479

commit v4 on v3

--- a/solution.py
+++ b/solution.py
@@ -13,7 +13,7 @@
 MOVE_BYTES = 40 * 1024 * 1024
 STORE_BYTES = 1024 * 1024
 RAW = 64
-SMALL = 4
+SMALL = 8
 LARGE = 5
 MINI = 16
 LAG = 2
@@ -225,7 +225,7 @@
         fetched(0, h, first, raw - first, ratio + h)
     for e in range(ratio, len(heads)):
         prepare_head(*heads[e])
-    held = len(heads) - ratio
+    held = len(heads) - 2 * ratio
     pl.semaphore_wait(barrier, n_row + n_col - 2)
     for e in range(held):
         begin_head(e)

time: 473 us -> 472 us (level)
  no operation moved by 1% of the time
where the time goes in v4:
time: 472 us; the launch traced here: 467 us
  Pallas kernels  466 us (99%)
    pallas_call x1, Pallas kernels, move_call(): pl.pallas_call(functools.partial(move_kernel, n_row, n_col, depth, RAW, h...  459 us

profile of v4, /device:TPU:5, one launch (start us, length us, event | category | flops | bytes accessed | tf_op | source)
XLA Modules:
  0.0 467.0 jit_solution(16754498806872152625)
XLA Ops:
  0.6 459.1 %shard_map.58 = (bf16[8,1152,1152]{2,1,0:T(8,128)(2,1)S(1)}, f32[2,9216]{1,0:T(2,128)S(1)}) custom-call(s32[2,4]{1,0:T(2,128)} %routes_ref.1, bf16[1152,4608]{1,0:T(8,128)(2,1)} %gate_ref.1, bf16[1152,4608]{1,0:T(8,128)(2,1)} %up_ref.1), custom_call_target="tpu_custom_call" | custom-call | tf_op jit(solution)/shard_map/pallas_call | solution.py:424
  459.8 7.2 %shard_map.59 = (bf16[576,9216]{1,0:T(8,128)(2,1)}, bf16[576,9216]{1,0:T(8,128)(2,1)}, f32[2,9216]{1,0:T(2,128)}) custom-call(bf16[8,1152,1152]{2,1,0:T(8,128)(2,1)S(1)} %get-tuple-element.5.got_ref, f32[2,9216]{1,0:T(2,128)S(1)} %get-tuple-element.6.scales_ref), custom_call_target="tpu_custom_call" | custom-call | tf_op jit(solution)/shard_map/pallas_call | solution.py:479
